TPU v7x, 32 devices: a whole 2x2x4 slice. The times are simulated.
32 devices in a mesh: parts: 2 (over y), ep: 16 (over z, x, core).
Axes of the slice: x: 2, y: 2, z: 4, core: 2. Of those that a mesh axis runs over, the one named last changes fastest.
Arguments:
- tokens: bfloat16 [512, 2048], P(('parts', 'ep')), parts along dimension 0, may hold values from -6 to 6
- gate_up: bfloat16 [4096, 16, 1536], P(('parts', 'ep')), parts along dimension 0, may hold values from -0.125 to 0.125
- down_proj: bfloat16 [1536, 16, 2048], P(('parts', 'ep')), parts along dimension 0, may hold values from -0.21875 to 0.21875
- expert_ids: int32 [512, 8], P(('parts', 'ep')), parts along dimension 0, may hold values from 0 to 15, all different within a row; in each aligned block of 16 rows (0 to 15, 16 to 31, ...) at most 16 rows name the same one
- gate_weights: float32 [512, 8], P(('parts', 'ep')), parts along dimension 0, may hold values from 0.03 to 0.6
- owner_slot: int32 [32], P('parts'), parts along dimension 0, may hold values from 0 to 15, each once
Outputs:
- moe_out: bfloat16 [512, 2048], P(('parts', 'ep')), parts along dimension 0
- channel_scale: float32 [32, 3584], P(('parts', 'ep')), parts along dimension 0
There are 2 independent parts, one for each index of `parts`. A program takes and returns all parts, laid end to end along the dimension named above; each array names one. Nothing has to cross between parts.
Inputs may be any that keep to these rules, and one draw needn't show every extreme that they name: `expert_ids`: each row names 8 different experts; among the rows of one device no expert is named more than 16 times, a bound that some block reaches. `owner_slot`: A permutation: each slot holds exactly one expert.
All inputs are finite; a program needn't handle non-finite values.
Results may differ from a plain program's by a relative error of at most 0.0058.
Values may be sent and summed in bfloat16 or wider, within the bound.
A program may use at most 128 MiB of HBM per device.

v0:
```python
import math

import jax
import jax.numpy as jnp
from jax import lax
from jax.sharding import PartitionSpec as P


def expert_block(arrived, held_up, held_down):
    hidden = jnp.einsum("rjd,djf->rjf", arrived, held_up, preferred_element_type=jnp.float32)
    ffn_width = held_up.shape[2] // 2
    activated = (jax.nn.silu(hidden[..., :ffn_width]) * hidden[..., ffn_width:]).astype(
        jnp.bfloat16
    )
    return jnp.einsum(
        "rjf,fjd->rjd", activated, held_down, preferred_element_type=jnp.float32
    ).astype(jnp.bfloat16)


def column_scales(gate_up, down_proj):
    gate_scale = jnp.max(jnp.abs(gate_up), axis=0).astype(jnp.float32) * math.sqrt(gate_up.shape[0])
    down_scale = jnp.max(jnp.abs(down_proj), axis=0).astype(jnp.float32) * math.sqrt(
        down_proj.shape[0]
    )
    return jnp.concatenate([gate_scale, down_scale], axis=1)


def shards(tokens, gate_up, down_proj, expert_ids, gate_weights, owner_slot):
    tok_rows, model_width = tokens.shape
    top_count = expert_ids.shape[1]
    slots_all = gate_up.shape[1]
    devices = lax.axis_size("ep")
    own_count = slots_all // devices
    capacity = 2 * tok_rows * top_count // slots_all
    experts_iota = jnp.arange(slots_all, dtype=jnp.int32)
    inverse = jnp.zeros((slots_all,), jnp.int32).at[owner_slot].set(experts_iota)
    flat_ids = expert_ids.reshape(-1)
    one_hot = (flat_ids[:, None] == experts_iota[None, :]).astype(jnp.int32)
    slot_rank = jnp.sum((jnp.cumsum(one_hot, axis=0) - 1) * one_hot, axis=1)
    position = slot_rank * slots_all + flat_ids
    source_rows = jnp.repeat(tokens, top_count, axis=0)
    outbox = (
        jnp.zeros((capacity * slots_all, model_width), jnp.bfloat16).at[position].set(source_rows)
    )
    outbox = outbox.reshape(capacity, slots_all, model_width)
    held_up, held_down = (
        lax.all_to_all(gate_up, "ep", split_axis=1, concat_axis=0, tiled=True),
        lax.all_to_all(down_proj, "ep", split_axis=1, concat_axis=0, tiled=True),
    )
    arrived = lax.all_to_all(outbox, "ep", split_axis=1, concat_axis=0, tiled=True)
    expert_out = expert_block(arrived, held_up, held_down)
    returned = lax.all_to_all(expert_out, "ep", split_axis=0, concat_axis=1, tiled=True).reshape(
        capacity * slots_all, model_width
    )
    picked = returned[position].astype(jnp.float32).reshape(tok_rows, top_count, model_width)
    moe_out = jnp.sum(picked * gate_weights[:, :, None], axis=1).astype(jnp.bfloat16)
    scales = column_scales(held_up, held_down)
    every_row = lax.all_gather(scales, "ep", axis=0, tiled=True)
    mine = lax.dynamic_slice_in_dim(inverse, lax.axis_index("ep") * own_count, own_count)
    scales = jnp.take(every_row, mine, axis=0)
    return (moe_out, scales)


def solution(mesh):
    in_specs = (
        P(("parts", "ep"), None),
        P(("parts", "ep"), None, None),
        P(("parts", "ep"), None, None),
        P(("parts", "ep"), None),
        P(("parts", "ep"), None),
        P("parts"),
    )
    out_specs = (P(("parts", "ep"), None), P(("parts", "ep"), None))
    return jax.shard_map(shards, mesh=mesh, in_specs=in_specs, out_specs=out_specs, check_vma=False)
```

profile of v0, /device:TPU:0, one launch (start us, length us, event | category | flops | bytes accessed | tf_op | source)
XLA Modules:
  0.0 311.9 jit_solution(7199482188254444874)
XLA Ops:
  0.6 0.8 copy.33
  1.4 0.1 eq.15
  1.5 0.1 reshape.118
  1.7 0.2 reduce_window_sum.11
  1.9 0.2 select_reduce_fusion
  2.1 1.7 scatter_custom_fusion
  3.8 1.6 copy.35
  5.4 7.4 %all-to-all-start = ((bf16[16,16,2048]{2,0,1:T(8,128)(2,1)}), bf16[16,16,2048]{2,0,1:T(8,128)(2,1)}, u32[]{:S(2)}, u32[]{:S(2)}) async-start(bf16[16,16,2048]{2,0,1:T(8,128)(2,1)} %copy.35), calls=%async_computation | async-start | bytes 2097152 | tf_op jit(solution)/shard_map/all_to_all | solution.py:50
  12.9 8.9 %copy.36 = bf16[128,16,1536]{2,0,1:T(8,128)(2,1)} copy(bf16[128,16,1536]{2,1,0:T(8,128)(2,1)} %param.7) | data formatting | bytes 12582912 | tf_op args[1]
  21.8 14.0 %all-to-all-done = bf16[16,16,2048]{2,0,1:T(8,128)(2,1)} async-done(((bf16[16,16,2048]{2,0,1:T(8,128)(2,1)}), bf16[16,16,2048]{2,0,1:T(8,128)(2,1)}, u32[]{:S(2)}, u32[]{:S(2)}) %all-to-all-start) | async-done | bytes 1048608 | tf_op jit(solution)/shard_map/all_to_all | solution.py:50
  35.8 6.8 %all-to-all-start.1 = ((bf16[128,16,1536]{2,0,1:T(8,128)(2,1)}), bf16[128,16,1536]{2,0,1:T(8,128)(2,1)}, u32[]{:S(2)}, u32[]{:S(2)}) async-start(bf16[128,16,1536]{2,0,1:T(8,128)(2,1)} %copy.36), calls=%async_computation.1 | async-start | bytes 12582912 | tf_op jit(solution)/shard_map/all_to_all | solution.py:47
  42.7 3.4 %copy.37 = bf16[48,16,2048]{2,0,1:T(8,128)(2,1)} copy(bf16[48,16,2048]{2,1,0:T(8,128)(2,1)S(1)} %copy-done.1) | data formatting | bytes 6291456 | tf_op args[2]
  46.1 110.7 %all-to-all-done.1 = bf16[128,16,1536]{2,0,1:T(8,128)(2,1)} async-done(((bf16[128,16,1536]{2,0,1:T(8,128)(2,1)}), bf16[128,16,1536]{2,0,1:T(8,128)(2,1)}, u32[]{:S(2)}, u32[]{:S(2)}) %all-to-all-start.1) | async-done | bytes 6291488 | tf_op jit(solution)/shard_map/all_to_all | solution.py:47
  156.7 28.1 %all-to-all-start.2 = ((bf16[48,16,2048]{2,0,1:T(8,128)(2,1)}), bf16[48,16,2048]{2,0,1:T(8,128)(2,1)S(1)}, u32[]{:S(2)}, u32[]{:S(2)}) async-start(bf16[48,16,2048]{2,0,1:T(8,128)(2,1)} %copy.37), calls=%async_computation.2 | async-start | bytes 6291456 | tf_op jit(solution)/shard_map/all_to_all | solution.py:48
  184.8 0.6 scatter_custom_fusion.1
  185.5 0.6 dynamic_slice.3
  188.1 6.1 %convolution_bitcast_fusion = f32[256,1,1536]{2,0,1:T(8,128)} fusion(bf16[256,2048]{1,0:T(8,128)(2,1)} %bitcast.6, bf16[2048,1536]{1,0:T(8,128)(2,1)} %bitcast.9), kind=kOutput, calls=%fused_computation.7 | convolution fusion | flops 1610612736 | bytes 8912896 | tf_op jit(solution)/shard_map/rjd,djf->rjf/dot_general | solution.py:10
  194.1 49.9 %all-to-all-done.2 = bf16[48,16,2048]{2,0,1:T(8,128)(2,1)S(1)} async-done(((bf16[48,16,2048]{2,0,1:T(8,128)(2,1)}), bf16[48,16,2048]{2,0,1:T(8,128)(2,1)S(1)}, u32[]{:S(2)}, u32[]{:S(2)}) %all-to-all-start.2) | async-done | bytes 3145760 | tf_op jit(solution)/shard_map/all_to_all | solution.py:48
  244.0 3.5 %fusion.2 = bf16[256,1,2048]{2,0,1:T(8,128)(2,1)} fusion(bf16[768,2048]{1,0:T(8,128)(2,1)S(1)} %bitcast.64, f32[256,1,1536]{2,0,1:T(8,128)} %convolution_bitcast_fusion), kind=kOutput, calls=%fused_computation.9 | convolution fusion | flops 807010304 | bytes 5767168 | tf_op jit(solution)/shard_map/rjf,fjd->rjd/dot_general | solution.py:15
  247.5 0.5 broadcast.120
  248.0 3.4 %reduce.4 = bf16[256,2048]{1,0:T(8,128)(2,1)} reduce(bf16[256,1,2048]{2,0,1:T(8,128)(2,1)} %fusion.2, bf16[]{:T(256)} %broadcast.120), dimensions={1}, to_apply=%copy.38.reduce_sub_computation | reduce | bytes 2097154 | tf_op jit(solution)/shard_map/convert_element_type | solution.py:17
  251.4 2.6 reshape.188
  254.0 15.5 %all-to-all-start.3 = ((bf16[16,2,16384]{2,1,0:T(2,128)(2,1)}), bf16[16,2,16384]{2,1,0:T(2,128)(2,1)}, u32[]{:S(2)}, u32[]{:S(2)}) async-start(bf16[16,2,16384]{2,1,0:T(2,128)(2,1)} %reshape.188), calls=%async_computation.3 | async-start | bytes 2097152 | tf_op jit(solution)/shard_map/all_to_all | solution.py:52
  269.5 0.3 fusion.1
  269.9 3.4 %fusion = bf16[1536]{0:T(1024)(128)(2,1)S(1)} fusion(bf16[128,16,1536]{2,0,1:T(8,128)(2,1)} %all-to-all-done.1), kind=kLoop, calls=%fused_computation.4 | loop fusion | flops 6289920 | bytes 6294528 | tf_op jit(solution)/shard_map/reduce_max | solution.py:21
  273.3 30.4 %all-gather = f32[16,1,3584]{2,1,0:T(1,128)S(1)} all-gather(f32[1,1,3584]{2,1,0:T(1,128)S(1)} %maximum_bitcast_fusion), channel_id=1, replica_groups=mesh['parts'=2,'ep'=16] {'ep'}, dimensions={0}, use_global_device_ids=true | all-gather | bytes 243712 | tf_op jit(solution)/shard_map/all_gather | solution.py:58
  303.8 0.6 fusion.12
  304.4 4.3 %reshape.189 = bf16[256,1,2048]{2,1,0:T(2,128)(2,1)S(1)} reshape(bf16[16,2,16384]{2,1,0:T(2,128)(2,1)} %all-to-all-done.3) | data formatting | bytes 2097152
  308.7 0.6 copy.41
  309.3 0.6 copy.39
  309.9 0.9 gather_fusion
  310.8 1.1 fusion.3
  (19 shorter events, 0.2 us)
Async XLA Ops:
  0.6 1.4 copy-start
  5.4 30.4 %all-to-all-start = ((bf16[16,16,2048]{2,0,1:T(8,128)(2,1)}), bf16[16,16,2048]{2,0,1:T(8,128)(2,1)}, u32[]{:S(2)}, u32[]{:S(2)}) async-start(bf16[16,16,2048]{2,0,1:T(8,128)(2,1)} %copy.35), calls=%async_computation | async-start | bytes 2097152 | tf_op jit(solution)/shard_map/all_to_all | solution.py:50
  21.8 20.9 %copy-start.1 = (bf16[48,16,2048]{2,1,0:T(8,128)(2,1)S(1)}, bf16[48,16,2048]{2,1,0:T(8,128)(2,1)}, u32[]{:S(2)}) copy-start(bf16[48,16,2048]{2,1,0:T(8,128)(2,1)} %param.8) | copy-start | bytes 9437188
  35.8 120.9 %all-to-all-start.1 = ((bf16[128,16,1536]{2,0,1:T(8,128)(2,1)}), bf16[128,16,1536]{2,0,1:T(8,128)(2,1)}, u32[]{:S(2)}, u32[]{:S(2)}) async-start(bf16[128,16,1536]{2,0,1:T(8,128)(2,1)} %copy.36), calls=%async_computation.1 | async-start | bytes 12582912 | tf_op jit(solution)/shard_map/all_to_all | solution.py:47
  46.1 138.7 %copy-start.3 = (s32[16]{0:T(128)S(1)}, s32[16]{0:T(128)}, u32[]{:S(2)}) copy-start(s32[16]{0:T(128)} %param.11) | copy-start | bytes 196
  46.1 141.9 %copy-start.2 = (f32[16,8]{0,1:T(8,128)S(1)}, f32[16,8]{0,1:T(8,128)}, u32[]{:S(2)}) copy-start(f32[16,8]{0,1:T(8,128)} %param.10) | copy-start | bytes 1540
  156.7 87.3 %all-to-all-start.2 = ((bf16[48,16,2048]{2,0,1:T(8,128)(2,1)}), bf16[48,16,2048]{2,0,1:T(8,128)(2,1)S(1)}, u32[]{:S(2)}, u32[]{:S(2)}) async-start(bf16[48,16,2048]{2,0,1:T(8,128)(2,1)} %copy.37), calls=%async_computation.2 | async-start | bytes 6291456 | tf_op jit(solution)/shard_map/all_to_all | solution.py:48
  254.0 50.4 %all-to-all-start.3 = ((bf16[16,2,16384]{2,1,0:T(2,128)(2,1)}), bf16[16,2,16384]{2,1,0:T(2,128)(2,1)}, u32[]{:S(2)}, u32[]{:S(2)}) async-start(bf16[16,2,16384]{2,1,0:T(2,128)(2,1)} %reshape.188), calls=%async_computation.3 | async-start | bytes 2097152 | tf_op jit(solution)/shard_map/all_to_all | solution.py:52
where the time goes:
time: 314 us; the launch traced here: 312 us
  waiting for transfers between devices  175 us (56%)
  starting transfers between devices  57.8 us (18%)
  blocking collectives  30.4 us (10%)
  local copies, waits for them, and re-layouts  27.5 us (9%)
  matrix products  9.51 us (3%)
  other arithmetic  9.31 us (3%)
    all_to_all x1, waiting for transfers between devices, shards(): lax.all_to_all(gate_up, 'ep', split_axis=1, concat_axis=0, tiled=True)  111 us
    all_to_all x1, waiting for transfers between devices, shards(): lax.all_to_all(down_proj, 'ep', split_axis=1, concat_axis=0, tiled=True)  49.9 us
    all_gather x1, blocking collectives, shards(): every_row = lax.all_gather(scales, 'ep', axis=0, tiled=True)  30.4 us
    all_to_all x1, starting transfers between devices, shards(): lax.all_to_all(down_proj, 'ep', split_axis=1, concat_axis=0, tiled=True)  28.1 us
    unnamed x15, local copies, waits for them, and re-layouts  20.7 us
    all_to_all x1, starting transfers between devices, shards(): lax.all_to_all(expert_out, 'ep', split_axis=0, concat_axis=1, tiled=True)  15.5 us
    all_to_all x1, waiting for transfers between devices, shards(): lax.all_to_all(outbox, 'ep', split_axis=1, concat_axis=0, tiled=True)  14 us
    all_to_all x1, starting transfers between devices, shards(): lax.all_to_all(outbox, 'ep', split_axis=1, concat_axis=0, tiled=True)  7.44 us
  transfers between devices with their start and end apart: 4, of which 3 were waited for; matrix products, arithmetic and copies ran while one was open for 8% of the time, Pallas kernels for 0%

commit v1 on v0

--- a/solution.py
+++ b/solution.py
@@ -1,8 +1,11 @@
+import functools
 import math
 
 import jax
 import jax.numpy as jnp
 from jax import lax
+from jax.experimental import pallas as pl
+from jax.experimental.pallas import tpu as pltpu
 from jax.sharding import PartitionSpec as P
 
 
@@ -61,6 +64,329 @@
     return (moe_out, scales)
 
 
+MESH = pl.DeviceIdType.MESH
+F32, BF16 = jnp.float32, jnp.bfloat16
+
+
+def fused_kernel(
+    dims, tok_ref, meta_ref, slot_ref, up_hbm, down_hbm, out_ref, scale_ref,
+    w_ref, wt_ref, d_ref, tok_all, tok_t, meta_all, meta_t, x_ref, h_ref, act_ref, a_ref,
+    o_ref, s_send, s_recv, *rest,
+):
+    n, bits, top, out_chunks = dims
+    hs, hr = rest[:bits], rest[bits : 2 * bits]
+    os_, or_ = rest[2 * bits : 3 * bits], rest[3 * bits : 4 * bits]
+    load_sem, small_send, small_recv, h_ssem, h_rsem, o_ssem, o_rsem = rest[4 * bits :]
+    me = lax.axis_index("ep")
+    own = tok_ref.shape[0]
+    total = tok_all.shape[0]
+    depth = tok_all.shape[1]
+    experts = slot_ref.shape[1]
+    half = w_ref.shape[1] // 2
+    fl = half // n
+    width = d_ref.shape[1]
+    root_d, root_f = math.sqrt(depth * n), math.sqrt(fl * n)
+
+    load_w = pltpu.make_async_copy(up_hbm, w_ref, load_sem.at[0])
+    load_d = pltpu.make_async_copy(down_hbm, d_ref, load_sem.at[1])
+    load_w.start()
+    load_d.start()
+
+    barrier = pltpu.get_barrier_semaphore()
+    for i in range(1, n):
+        pl.semaphore_signal(
+            barrier, inc=1, device_id={"ep": lax.rem(me + i, n)}, device_id_type=MESH
+        )
+    pl.semaphore_wait(barrier, n - 1)
+
+    def remote(src, dst, ssem, rsem, peer):
+        return pltpu.make_async_remote_copy(
+            src_ref=src, dst_ref=dst, send_sem=ssem, recv_sem=rsem,
+            device_id={"ep": peer}, device_id_type=MESH,
+        )
+
+    mine = pl.ds(pl.multiple_of(me * own, own), own)
+
+    def tok_copy(i):
+        peer = lax.rem(me + i, n)
+        cols = pl.ds(pl.multiple_of(peer * depth, depth), depth)
+        return remote(
+            tok_ref.at[:, cols], tok_all.at[mine, :], small_send.at[0, i], small_recv.at[0, i], peer
+        )
+
+    def meta_copy(i):
+        peer = lax.rem(me + i, n)
+        return remote(
+            meta_ref, meta_all.at[mine, :], small_send.at[1, i], small_recv.at[1, i], peer
+        )
+
+    def scale_copy(i):
+        peer = lax.rem(me + i, n)
+        return remote(
+            s_send.at[peer], s_recv.at[me], small_send.at[2, i], small_recv.at[2, i], peer
+        )
+
+    for i in range(1, n):
+        meta_copy(i).start()
+        tok_copy(i).start()
+    tok_all[mine, :] = tok_ref[:, pl.ds(pl.multiple_of(me * depth, depth), depth)]
+    meta_all[mine, :] = meta_ref[...]
+    a_ref[...] = jnp.zeros_like(a_ref)
+
+    load_w.wait()
+    tile = 2 * depth
+
+    @pl.loop(0, w_ref.shape[1] // tile)
+    def _(c):
+        cols = pl.ds(pl.multiple_of(c * tile, tile), tile)
+
+        @pl.loop(0, w_ref.shape[0] // tile)
+        def _(r):
+            rows = pl.ds(pl.multiple_of(r * tile, tile), tile)
+            wt_ref[cols, rows] = w_ref[rows, cols].T
+
+    for i in range(1, n):
+        meta_copy(i).wait_recv()
+        tok_copy(i).wait_recv()
+    tok_t[...] = tok_all[...].astype(F32).T
+    meta_t[...] = meta_all[...].T
+
+    lanes = lax.broadcasted_iota(jnp.int32, (experts, total), 0).astype(F32)
+
+    def mask_of(k):
+        return meta_t[pl.ds(k, 1), :] == lanes
+
+    def partner(s):
+        bit = 1 << s
+        return me + bit * (1 - 2 * lax.rem(me // bit, 2))
+
+    def h_copy(k, s):
+        return remote(hs[s].at[k], hr[s].at[k], h_ssem.at[s, k], h_rsem.at[s, k], partner(s))
+
+    def o_copy(q, s):
+        return remote(os_[s].at[q], or_[s].at[q], o_ssem.at[s, q], o_rsem.at[s, q], partner(s))
+
+    def h_rows(k, j, part):
+        return h_ref[k, pl.ds(pl.multiple_of(part * half + j * fl, 16), fl), :]
+
+    def h_sum(k, j, s, part):
+        total_ = h_rows(k, j, part)
+        for prior in range(s):
+            total_ += hr[prior][k, j // (2 << prior), pl.ds(part * fl, fl), :].astype(F32)
+        return total_
+
+    def product(k):
+        mask = mask_of(k)
+
+        @pl.loop(0, depth // 8)
+        def _(block):
+            for inner in range(8):
+                d = block * 8 + inner
+                row = jnp.where(mask, tok_t[pl.ds(d, 1), :], 0.0)
+                x_ref[pl.ds(pl.multiple_of(d * experts, experts), experts), :] = row.astype(BF16)
+
+        @pl.loop(0, wt_ref.shape[0] // tile)
+        def _(r):
+            rows = pl.ds(pl.multiple_of(r * tile, tile), tile)
+            h_ref[k, rows, :] = jnp.dot(wt_ref[rows, :], x_ref[...], preferred_element_type=F32)
+
+    def h_send(k, s):
+        if s > 0:
+            h_copy(k, s - 1).wait_recv()
+        bit = 1 << s
+        base = (1 - lax.rem(me // bit, 2)) * bit + lax.rem(me, bit)
+        for m in range(n // (2 * bit)):
+            j = m * 2 * bit + base
+            for part in range(2):
+                hs[s][k, m, pl.ds(part * fl, fl), :] = h_sum(k, j, s, part).astype(BF16)
+        h_copy(k, s).start()
+
+    def h_final(k):
+        h_copy(k, bits - 1).wait_recv()
+        gate = h_sum(k, me, bits, 0)
+        act = gate / (1.0 + jnp.exp(-gate)) * h_sum(k, me, bits, 1)
+        act_ref[...] = act * meta_t[pl.ds(top + k, 1), :]
+        mask = mask_of(k)
+
+        @pl.loop(0, fl // 8)
+        def _(block):
+            for inner in range(8):
+                f = block * 8 + inner
+                rows = pl.ds(pl.multiple_of(f * experts, experts), experts)
+                a_ref[rows, :] += jnp.where(mask, act_ref[pl.ds(f, 1), :], 0.0)
+
+    def scales_out():
+        def up_max(r, best):
+            rows = pl.ds(pl.multiple_of(r * experts, experts), experts)
+            return jnp.maximum(best, jnp.abs(w_ref[rows, :]))
+
+        def down_max(r, best):
+            rows = pl.ds(pl.multiple_of(r * experts, experts), experts)
+            return jnp.maximum(best, jnp.abs(d_ref[rows, :]))
+
+        choose = (
+            lax.broadcasted_iota(jnp.int32, (experts, experts), 0)
+            == jnp.broadcast_to(slot_ref[...], (experts, experts))
+        ).astype(F32).astype(BF16)
+        best = lax.fori_loop(0, depth, up_max, jnp.zeros((experts, 2 * half), BF16))
+        up = jnp.dot(choose, best, preferred_element_type=F32)
+        load_d.wait()
+        best = lax.fori_loop(0, fl, down_max, jnp.zeros((experts, width), BF16))
+        down = jnp.dot(choose, best, preferred_element_type=F32)
+        for slot in range(experts):
+            s_send[slot, :, pl.ds(0, 2 * half)] = up[slot : slot + 1]
+            s_send[slot, :, pl.ds(2 * half, width)] = down[slot : slot + 1]
+        for i in range(1, n):
+            scale_copy(i).start()
+        s_recv[me] = s_send[me]
+
+    @pl.loop(0, top + bits)
+    def _(step):
+        @pl.when(step < top)
+        def _():
+            product(step)
+            h_send(step, 0)
+
+        for s in range(1, bits):
+            @pl.when((step >= s) & (step < top + s))
+            def _():
+                h_send(step - s, s)
+
+        @pl.when(step >= bits)
+        def _():
+            h_final(step - bits)
+
+        @pl.when(step == 0)
+        def _():
+            scales_out()
+
+    cols_out = width // out_chunks
+    a_t = a_ref[...].T.astype(BF16)
+
+    def o_sum(q, j, s):
+        total_ = o_ref[q, pl.ds(pl.multiple_of(j * own, own), own), :]
+        for prior in range(s):
+            total_ += or_[prior][q, j // (2 << prior)].astype(F32)
+        return total_
+
+    def o_send(q, s):
+        if s > 0:
+            o_copy(q, s - 1).wait_recv()
+        bit = 1 << s
+        base = (1 - lax.rem(me // bit, 2)) * bit + lax.rem(me, bit)
+        for m in range(n // (2 * bit)):
+            os_[s][q, m] = o_sum(q, m * 2 * bit + base, s).astype(BF16)
+        o_copy(q, s).start()
+
+    for step in range(out_chunks + bits):
+        if step < out_chunks:
+            o_ref[step] = jnp.dot(
+                a_t, d_ref[:, pl.ds(step * cols_out, cols_out)], preferred_element_type=F32
+            )
+            o_send(step, 0)
+        for s in range(1, bits):
+            if s <= step < out_chunks + s:
+                o_send(step - s, s)
+        if step >= bits:
+            q = step - bits
+            o_copy(q, bits - 1).wait_recv()
+            out_ref[:, pl.ds(q * cols_out, cols_out)] = o_sum(q, me, bits).astype(BF16)
+
+    for i in range(1, n):
+        scale_copy(i).wait_recv()
+    best = s_recv[0]
+    for i in range(1, n):
+        best = jnp.maximum(best, s_recv[i])
+    scale_ref[:, pl.ds(0, 2 * half)] = best[:, : 2 * half] * root_d
+    scale_ref[:, pl.ds(2 * half, width)] = best[:, 2 * half :] * root_f
+    for i in range(1, n):
+        meta_copy(i).wait_send()
+        tok_copy(i).wait_send()
+        scale_copy(i).wait_send()
+
+    @pl.loop(0, top)
+    def _(k):
+        for s in range(bits):
+            h_copy(k, s).wait_send()
+
+    for q in range(out_chunks):
+        for s in range(bits):
+            o_copy(q, s).wait_send()
+
+
+def fused(tokens, gate_up, down_proj, expert_ids, gate_weights, owner_slot):
+    n = lax.axis_size("ep")
+    bits = n.bit_length() - 1
+    own, width = tokens.shape
+    depth, experts, both = gate_up.shape
+    fl = down_proj.shape[0]
+    top = expert_ids.shape[1]
+    total = own * n
+    out_chunks = 2
+    meta = jnp.concatenate([expert_ids.astype(F32), gate_weights], axis=1)
+    meta = jnp.pad(meta, ((0, 0), (0, 128 - 2 * top)))
+    vmem = pl.BlockSpec(memory_space=pltpu.VMEM)
+    hbm = pl.BlockSpec(memory_space=pl.ANY)
+    counts = [n >> (s + 1) for s in range(bits)]
+    hidden_bufs = [pltpu.VMEM((top, c, 2 * fl, total), BF16) for c in counts]
+    out_bufs = [pltpu.VMEM((out_chunks, c, own, width // out_chunks), BF16) for c in counts]
+    return pl.pallas_call(
+        functools.partial(fused_kernel, (n, bits, top, out_chunks)),
+        out_shape=(
+            jax.ShapeDtypeStruct((own, width), BF16),
+            jax.ShapeDtypeStruct((1, both + width), F32),
+        ),
+        in_specs=[vmem, vmem, vmem, hbm, hbm],
+        out_specs=(vmem, vmem),
+        scratch_shapes=[
+            pltpu.VMEM((depth * experts, both), BF16),
+            pltpu.VMEM((both, depth * experts), BF16),
+            pltpu.VMEM((fl * experts, width), BF16),
+            pltpu.VMEM((total, depth), BF16),
+            pltpu.VMEM((depth, total), F32),
+            pltpu.VMEM((total, 128), F32),
+            pltpu.VMEM((128, total), F32),
+            pltpu.VMEM((depth * experts, total), BF16),
+            pltpu.VMEM((top, both, total), F32),
+            pltpu.VMEM((fl, total), F32),
+            pltpu.VMEM((fl * experts, total), F32),
+            pltpu.VMEM((out_chunks, total, width // out_chunks), F32),
+            pltpu.VMEM((n, 1, both + width), F32),
+            pltpu.VMEM((n, 1, both + width), F32),
+            *hidden_bufs, *hidden_bufs, *out_bufs, *out_bufs,
+            pltpu.SemaphoreType.DMA((2,)),
+            pltpu.SemaphoreType.DMA((3, n)),
+            pltpu.SemaphoreType.DMA((3, n)),
+            pltpu.SemaphoreType.DMA((bits, top)),
+            pltpu.SemaphoreType.DMA((bits, top)),
+            pltpu.SemaphoreType.DMA((bits, out_chunks)),
+            pltpu.SemaphoreType.DMA((bits, out_chunks)),
+        ],
+        compiler_params=pltpu.CompilerParams(
+            collective_id=0, has_side_effects=True, vmem_limit_bytes=60 * 2**20
+        ),
+    )(
+        tokens,
+        meta,
+        owner_slot.reshape(1, experts),
+        gate_up.reshape(depth * experts, both),
+        down_proj.reshape(fl * experts, width),
+    )
+
+
+def layer(tokens, gate_up, down_proj, expert_ids, gate_weights, owner_slot):
+    n = lax.axis_size("ep")
+    own = tokens.shape[0]
+    depth, experts, both = gate_up.shape
+    partials = n * own * expert_ids.shape[1] * both
+    aligned = (
+        n & (n - 1) == 0 and depth % 128 == 0 and experts == n and experts % 16 == 0
+        and down_proj.shape[0] % 16 == 0 and own % 16 == 0
+    )
+    args = (tokens, gate_up, down_proj, expert_ids, gate_weights, owner_slot)
+    return fused(*args) if aligned and partials <= gate_up.size else shards(*args)
+
+
 def solution(mesh):
     in_specs = (
         P(("parts", "ep"), None),
@@ -71,4 +397,4 @@
         P("parts"),
     )
     out_specs = (P(("parts", "ep"), None), P(("parts", "ep"), None))
-    return jax.shard_map(shards, mesh=mesh, in_specs=in_specs, out_specs=out_specs, check_vma=False)
+    return jax.shard_map(layer, mesh=mesh, in_specs=in_specs, out_specs=out_specs, check_vma=False)

time: 314 us -> 91.2 us (0.29)
  waiting for transfers between devices: 175 us -> 0 us
  Pallas kernels: 0 us -> 85.2 us
  starting transfers between devices: 57.8 us -> 0 us
  blocking collectives: 30.4 us -> 0 us
  local copies, waits for them, and re-layouts: 27.5 us -> 3.62 us
  matrix products: 9.51 us -> 0 us
  other arithmetic: 9.31 us -> 1.37 us
    all_to_all x4 -> x0, waiting for transfers between devices: 175 us -> none  [the longest x1 111 us: shards(): lax.all_to_all(gate_up, 'ep', split_axis=1, concat_axis=0, tiled=True)]
    pallas_call x0 -> x1, Pallas kernels: none -> 85.2 us  [fused(): pl.pallas_call(functools.partial(fused_kernel, (n, bits, top, out_chunks)...]
    all_to_all x4 -> x0, starting transfers between devices: 57.8 us -> none  [the longest x1 28.1 us: shards(): lax.all_to_all(down_proj, 'ep', split_axis=1, concat_axis=0, tiled=True)]
    all_gather x1 -> x0, blocking collectives: 30.4 us -> none  [shards(): every_row = lax.all_gather(scales, 'ep', axis=0, tiled=True)]
    unnamed x15 -> x3, local copies, waits for them, and re-layouts: 20.7 us -> 3.54 us
    dot_general x2 -> x0, matrix products: 9.51 us -> none  [the longest x1 6.05 us: expert_block(): jnp.einsum('rjd,djf->rjf', arrived, held_up, preferred_element_type=jnp.f...]
    reduce_max x2 -> x0, other arithmetic: 3.76 us -> none  [the longest x1 3.42 us: column_scales(): jnp.max(jnp.abs(gate_up), axis=0).astype(jnp.float32)]
  transfers between devices with their start and end apart: 4 -> 0, of which waited for: 3 -> 0; matrix products, arithmetic and copies ran while one was open for 8% -> 0% of each run, Pallas kernels for 0% -> 0%
where the time goes in v1:
time: 91.2 us; the launch traced here: 90.9 us
  Pallas kernels  85.2 us (93%)
  local copies, waits for them, and re-layouts  3.62 us (4%)
  other arithmetic  1.37 us (2%)
    pallas_call x1, Pallas kernels, fused(): pl.pallas_call(functools.partial(fused_kernel, (n, bits, top, out_chunks)...  85.2 us
    unnamed x3, local copies, waits for them, and re-layouts  3.54 us

profile of v1, /device:TPU:0, one launch (start us, length us, event | category | flops | bytes accessed | tf_op | source)
XLA Modules:
  0.0 90.9 jit_solution(6529116974054639499)
XLA Ops:
  0.6 0.7 convert_element_type.5
  1.3 0.1 copy.10
  1.4 0.8 copy.11
  2.2 0.7 select_maximum_fusion.meta_ref
  2.8 85.2 %shard_map.77 = (bf16[16,2048]{1,0:T(8,128)(2,1)}, f32[1,3584]{1,0:T(1,128)}) custom-call(bf16[16,2048]{1,0:T(8,128)(2,1)} %tok_ref.1, f32[16,128]{1,0:T(8,128)} %select_maximum_fusion.meta_ref, s32[1,16]{1,0:T(1,128)} %bitcast.5, bf16[2048,1536]{1,0:T(8,128)(2,1)} %bitcast.3, bf16[768,2048]{1,0:T(8,128)(2,1)} %bitcast.4), custom_call_target="tpu_custom_call" | custom-call | tf_op jit(solution)/shard_map/pallas_call | solution.py:333
  88.1 1.5 %copy.14 = bf16[16,2048]{1,0:T(8,128)(2,1)} copy(bf16[16,2048]{1,0:T(8,128)(2,1)} %get-tuple-element.4) | data formatting | bytes 131072
  89.6 1.3 %copy.15 = f32[1,3584]{1,0:T(1,128)} copy(f32[1,3584]{1,0:T(1,128)} %get-tuple-element.5) | data formatting | bytes 28672

commit v2 on v1

--- a/solution.py
+++ b/solution.py
@@ -69,11 +69,11 @@
 
 
 def fused_kernel(
-    dims, tok_ref, meta_ref, slot_ref, up_hbm, down_hbm, out_ref, scale_ref,
-    w_ref, wt_ref, d_ref, tok_all, tok_t, meta_all, meta_t, x_ref, h_ref, act_ref, a_ref,
-    o_ref, s_send, s_recv, *rest,
+    dims, tok_ref, ids_ref, gate_ref, slot_ref, up_hbm, down_hbm, out_ref, scale_ref,
+    w_ref, wt_ref, d_ref, meta32, meta_ref, tok_all, tok_t, meta_all, id_row, gate_row, x_ref,
+    h_ref, act_ref, a_ref, o_ref, out32, s_send, s_recv, *rest,
 ):
-    n, bits, top, out_chunks = dims
+    n, bits, chunks, groups = dims
     hs, hr = rest[:bits], rest[bits : 2 * bits]
     os_, or_ = rest[2 * bits : 3 * bits], rest[3 * bits : 4 * bits]
     load_sem, small_send, small_recv, h_ssem, h_rsem, o_ssem, o_rsem = rest[4 * bits :]
@@ -82,6 +82,11 @@
     total = tok_all.shape[0]
     depth = tok_all.shape[1]
     experts = slot_ref.shape[1]
+    top = ids_ref.shape[1]
+    per = chunks // groups
+    span = total // groups
+    copies = total // span
+    small = own // groups
     half = w_ref.shape[1] // 2
     fl = half // n
     width = d_ref.shape[1]
@@ -91,6 +96,15 @@
     load_d = pltpu.make_async_copy(down_hbm, d_ref, load_sem.at[1])
     load_w.start()
     load_d.start()
+
+    meta32[...] = jnp.zeros_like(meta32)
+    gates = gate_ref[...]
+    meta32[:, 0:top] = ids_ref[...].astype(F32)
+    for piece in range(1, 4):
+        high = gates.astype(BF16).astype(F32)
+        meta32[:, piece * top : (piece + 1) * top] = high
+        gates = gates - high
+    meta_ref[...] = meta32[...].astype(BF16)
 
     barrier = pltpu.get_barrier_semaphore()
     for i in range(1, n):
@@ -133,89 +147,7 @@
     meta_all[mine, :] = meta_ref[...]
     a_ref[...] = jnp.zeros_like(a_ref)
 
-    load_w.wait()
-    tile = 2 * depth
-
-    @pl.loop(0, w_ref.shape[1] // tile)
-    def _(c):
-        cols = pl.ds(pl.multiple_of(c * tile, tile), tile)
-
-        @pl.loop(0, w_ref.shape[0] // tile)
-        def _(r):
-            rows = pl.ds(pl.multiple_of(r * tile, tile), tile)
-            wt_ref[cols, rows] = w_ref[rows, cols].T
-
-    for i in range(1, n):
-        meta_copy(i).wait_recv()
-        tok_copy(i).wait_recv()
-    tok_t[...] = tok_all[...].astype(F32).T
-    meta_t[...] = meta_all[...].T
-
-    lanes = lax.broadcasted_iota(jnp.int32, (experts, total), 0).astype(F32)
-
-    def mask_of(k):
-        return meta_t[pl.ds(k, 1), :] == lanes
-
-    def partner(s):
-        bit = 1 << s
-        return me + bit * (1 - 2 * lax.rem(me // bit, 2))
-
-    def h_copy(k, s):
-        return remote(hs[s].at[k], hr[s].at[k], h_ssem.at[s, k], h_rsem.at[s, k], partner(s))
-
-    def o_copy(q, s):
-        return remote(os_[s].at[q], or_[s].at[q], o_ssem.at[s, q], o_rsem.at[s, q], partner(s))
-
-    def h_rows(k, j, part):
-        return h_ref[k, pl.ds(pl.multiple_of(part * half + j * fl, 16), fl), :]
-
-    def h_sum(k, j, s, part):
-        total_ = h_rows(k, j, part)
-        for prior in range(s):
-            total_ += hr[prior][k, j // (2 << prior), pl.ds(part * fl, fl), :].astype(F32)
-        return total_
-
-    def product(k):
-        mask = mask_of(k)
-
-        @pl.loop(0, depth // 8)
-        def _(block):
-            for inner in range(8):
-                d = block * 8 + inner
-                row = jnp.where(mask, tok_t[pl.ds(d, 1), :], 0.0)
-                x_ref[pl.ds(pl.multiple_of(d * experts, experts), experts), :] = row.astype(BF16)
-
-        @pl.loop(0, wt_ref.shape[0] // tile)
-        def _(r):
-            rows = pl.ds(pl.multiple_of(r * tile, tile), tile)
-            h_ref[k, rows, :] = jnp.dot(wt_ref[rows, :], x_ref[...], preferred_element_type=F32)
-
-    def h_send(k, s):
-        if s > 0:
-            h_copy(k, s - 1).wait_recv()
-        bit = 1 << s
-        base = (1 - lax.rem(me // bit, 2)) * bit + lax.rem(me, bit)
-        for m in range(n // (2 * bit)):
-            j = m * 2 * bit + base
-            for part in range(2):
-                hs[s][k, m, pl.ds(part * fl, fl), :] = h_sum(k, j, s, part).astype(BF16)
-        h_copy(k, s).start()
-
-    def h_final(k):
-        h_copy(k, bits - 1).wait_recv()
-        gate = h_sum(k, me, bits, 0)
-        act = gate / (1.0 + jnp.exp(-gate)) * h_sum(k, me, bits, 1)
-        act_ref[...] = act * meta_t[pl.ds(top + k, 1), :]
-        mask = mask_of(k)
-
-        @pl.loop(0, fl // 8)
-        def _(block):
-            for inner in range(8):
-                f = block * 8 + inner
-                rows = pl.ds(pl.multiple_of(f * experts, experts), experts)
-                a_ref[rows, :] += jnp.where(mask, act_ref[pl.ds(f, 1), :], 0.0)
-
-    def scales_out():
+    def scales_in():
         def up_max(r, best):
             rows = pl.ds(pl.multiple_of(r * experts, experts), experts)
             return jnp.maximum(best, jnp.abs(w_ref[rows, :]))
@@ -236,62 +168,171 @@
         for slot in range(experts):
             s_send[slot, :, pl.ds(0, 2 * half)] = up[slot : slot + 1]
             s_send[slot, :, pl.ds(2 * half, width)] = down[slot : slot + 1]
-        for i in range(1, n):
-            scale_copy(i).start()
         s_recv[me] = s_send[me]
 
-    @pl.loop(0, top + bits)
+    load_w.wait()
+    tile = 2 * depth
+
+    @pl.loop(0, w_ref.shape[1] // tile)
+    def _(c):
+        cols = pl.ds(pl.multiple_of(c * tile, tile), tile)
+
+        @pl.loop(0, w_ref.shape[0] // tile)
+        def _(r):
+            rows = pl.ds(pl.multiple_of(r * tile, tile), tile)
+            wt_ref[cols, rows] = w_ref[rows, cols].T
+
+    scales_in()
+    for i in range(1, n):
+        meta_copy(i).wait_recv()
+        tok_copy(i).wait_recv()
+
+    row = lax.broadcasted_iota(jnp.int32, (total, total), 0)
+    col = lax.broadcasted_iota(jnp.int32, (total, total), 1)
+    source = (lax.rem(row, span) // small) * own + (row // span) * small + lax.rem(row, small)
+    order = (source == col).astype(F32).astype(BF16)
+    tok_p = jnp.dot(order, tok_all[...], preferred_element_type=F32).T
+    meta_p = jnp.dot(order, meta_all[...], preferred_element_type=F32).T
+    gate_p = meta_p[top : 2 * top] + meta_p[2 * top : 3 * top] + meta_p[3 * top : 4 * top]
+    for g in range(groups):
+        lo, hi = g * span, (g + 1) * span
+        for c in range(copies):
+            tok_t[g, :, c * span : (c + 1) * span] = tok_p[:, lo:hi]
+            for chunk in range(per):
+                k, at = chunk * copies + c, g * per + chunk
+                id_row[at : at + 1, c * span : (c + 1) * span] = meta_p[k : k + 1, lo:hi]
+                gate_row[at : at + 1, c * span : (c + 1) * span] = gate_p[k : k + 1, lo:hi]
+
+    lanes = lax.broadcasted_iota(jnp.int32, (experts, total), 0).astype(F32)
+
+    def mask_of(k):
+        return id_row[pl.ds(k, 1), :] == lanes
+
+    def partner(s):
+        bit = 1 << s
+        return me + bit * (1 - 2 * lax.rem(me // bit, 2))
+
+    def h_copy(k, s):
+        return remote(hs[s].at[k], hr[s].at[k], h_ssem.at[s, k], h_rsem.at[s, k], partner(s))
+
+    def o_copy(q, s):
+        return remote(os_[s].at[q], or_[s].at[q], o_ssem.at[s, q], o_rsem.at[s, q], partner(s))
+
+    def h_rows(k, j, part):
+        return h_ref[k, pl.ds(pl.multiple_of(part * half + j * fl, 16), fl), :]
+
+    def h_sum(k, j, s, part):
+        total_ = h_rows(k, j, part)
+        for prior in range(s):
+            total_ += hr[prior][k, j // (2 << prior), pl.ds(part * fl, fl), :].astype(F32)
+        return total_
+
+    def product(k):
+        mask = mask_of(k)
+
+        @pl.loop(0, depth // 8)
+        def _(block):
+            for inner in range(8):
+                d = block * 8 + inner
+                row = jnp.where(mask, tok_t[k // per, pl.ds(d, 1), :], 0.0)
+                x_ref[pl.ds(pl.multiple_of(d * experts, experts), experts), :] = row.astype(BF16)
+
+        h_ref[k] = jnp.dot(wt_ref[...], x_ref[...], preferred_element_type=F32)
+
+    def h_send(k, s):
+        if s > 0:
+            h_copy(k, s - 1).wait_recv()
+        bit = 1 << s
+        base = (1 - lax.rem(me // bit, 2)) * bit + lax.rem(me, bit)
+        for m in range(n // (2 * bit)):
+            j = m * 2 * bit + base
+            for part in range(2):
+                hs[s][k, m, pl.ds(part * fl, fl), :] = h_sum(k, j, s, part).astype(hs[s].dtype)
+        h_copy(k, s).start()
+
+    def h_final(k):
+        h_copy(k, bits - 1).wait_recv()
+        gate = h_sum(k, me, bits, 0)
+        act = gate / (1.0 + jnp.exp(-gate)) * h_sum(k, me, bits, 1)
+        act_ref[...] = act * gate_row[pl.ds(k, 1), :]
+        mask = mask_of(k)
+
+        @pl.loop(0, fl // 8)
+        def _(block):
+            for inner in range(8):
+                f = block * 8 + inner
+                rows = pl.ds(pl.multiple_of(f * experts, experts), experts)
+                placed = jnp.where(mask, act_ref[pl.ds(f, 1), :], 0.0)
+                for c in range(copies):
+                    a_ref[k // per, rows, :] += placed[:, c * span : (c + 1) * span]
+
+    def o_sum(g, j, s):
+        total_ = o_ref[g, pl.ds(pl.multiple_of(j * small, small), small), :]
+        for prior in range(s):
+            total_ += or_[prior][g, j // (2 << prior)].astype(F32)
+        return total_
+
+    def o_product(g):
+        a_t = a_ref[g].T.astype(BF16)
+        wide = width // 4
+
+        @pl.loop(0, 4)
+        def _(c):
+            cols = pl.ds(pl.multiple_of(c * wide, wide), wide)
+            o_ref[g, :, cols] = jnp.dot(a_t, d_ref[:, cols], preferred_element_type=F32)
+
+    def o_send(g, s):
+        if s > 0:
+            o_copy(g, s - 1).wait_recv()
+        bit = 1 << s
+        base = (1 - lax.rem(me // bit, 2)) * bit + lax.rem(me, bit)
+        for m in range(n // (2 * bit)):
+            os_[s][g, m] = o_sum(g, m * 2 * bit + base, s).astype(os_[s].dtype)
+        o_copy(g, s).start()
+
+    def o_final(g):
+        o_copy(g, bits - 1).wait_recv()
+        out32[pl.ds(pl.multiple_of(g * small, small), small), :] = o_sum(g, me, bits)
+
+    lags = [s + (s > 1) for s in range(bits + 1)]
+    late = lags[bits]
+    lead = per - 1 + late
+
+    @pl.loop(0, (groups - 1) * per + lead + late + 1)
     def _(step):
-        @pl.when(step < top)
+        @pl.when(step < chunks)
         def _():
             product(step)
             h_send(step, 0)
 
         for s in range(1, bits):
-            @pl.when((step >= s) & (step < top + s))
+            @pl.when((step >= lags[s]) & (step < chunks + lags[s]))
             def _():
-                h_send(step - s, s)
-
-        @pl.when(step >= bits)
+                h_send(step - lags[s], s)
+
+        @pl.when((step >= late) & (step < chunks + late))
         def _():
-            h_final(step - bits)
-
-        @pl.when(step == 0)
+            h_final(step - late)
+
+        for s in range(bits + 1):
+            since = step - lead - lags[s]
+
+            @pl.when((since >= 0) & (lax.rem(since + per * (late + chunks), per) == 0) & (since < chunks))
+            def _():
+                g = since // per
+                if s == 0:
+                    o_product(g)
+                if s < bits:
+                    o_send(g, s)
+                else:
+                    o_final(g)
+
+        @pl.when(step == 1)
         def _():
-            scales_out()
-
-    cols_out = width // out_chunks
-    a_t = a_ref[...].T.astype(BF16)
-
-    def o_sum(q, j, s):
-        total_ = o_ref[q, pl.ds(pl.multiple_of(j * own, own), own), :]
-        for prior in range(s):
-            total_ += or_[prior][q, j // (2 << prior)].astype(F32)
-        return total_
-
-    def o_send(q, s):
-        if s > 0:
-            o_copy(q, s - 1).wait_recv()
-        bit = 1 << s
-        base = (1 - lax.rem(me // bit, 2)) * bit + lax.rem(me, bit)
-        for m in range(n // (2 * bit)):
-            os_[s][q, m] = o_sum(q, m * 2 * bit + base, s).astype(BF16)
-        o_copy(q, s).start()
-
-    for step in range(out_chunks + bits):
-        if step < out_chunks:
-            o_ref[step] = jnp.dot(
-                a_t, d_ref[:, pl.ds(step * cols_out, cols_out)], preferred_element_type=F32
-            )
-            o_send(step, 0)
-        for s in range(1, bits):
-            if s <= step < out_chunks + s:
-                o_send(step - s, s)
-        if step >= bits:
-            q = step - bits
-            o_copy(q, bits - 1).wait_recv()
-            out_ref[:, pl.ds(q * cols_out, cols_out)] = o_sum(q, me, bits).astype(BF16)
-
+            for i in range(1, n):
+                scale_copy(i).start()
+
+    out_ref[...] = out32[...].astype(BF16)
     for i in range(1, n):
         scale_copy(i).wait_recv()
     best = s_recv[0]
@@ -304,14 +345,14 @@
         tok_copy(i).wait_send()
         scale_copy(i).wait_send()
 
-    @pl.loop(0, top)
+    @pl.loop(0, chunks)
     def _(k):
         for s in range(bits):
             h_copy(k, s).wait_send()
 
-    for q in range(out_chunks):
+    for g in range(groups):
         for s in range(bits):
-            o_copy(q, s).wait_send()
+            o_copy(g, s).wait_send()
 
 
 def fused(tokens, gate_up, down_proj, expert_ids, gate_weights, owner_slot):
@@ -322,52 +363,58 @@
     fl = down_proj.shape[0]
     top = expert_ids.shape[1]
     total = own * n
-    out_chunks = 2
-    meta = jnp.concatenate([expert_ids.astype(F32), gate_weights], axis=1)
-    meta = jnp.pad(meta, ((0, 0), (0, 128 - 2 * top)))
+    groups = 2
+    chunks = top
+    span = total // groups
     vmem = pl.BlockSpec(memory_space=pltpu.VMEM)
     hbm = pl.BlockSpec(memory_space=pl.ANY)
     counts = [n >> (s + 1) for s in range(bits)]
-    hidden_bufs = [pltpu.VMEM((top, c, 2 * fl, total), BF16) for c in counts]
-    out_bufs = [pltpu.VMEM((out_chunks, c, own, width // out_chunks), BF16) for c in counts]
+    kinds = [BF16 if s else F32 for s in range(bits)]
+    hidden_bufs = [pltpu.VMEM((chunks, c, 2 * fl, total), t) for c, t in zip(counts, kinds)]
+    out_bufs = [pltpu.VMEM((groups, c, own // groups, width), t) for c, t in zip(counts, kinds)]
     return pl.pallas_call(
-        functools.partial(fused_kernel, (n, bits, top, out_chunks)),
+        functools.partial(fused_kernel, (n, bits, chunks, groups)),
         out_shape=(
             jax.ShapeDtypeStruct((own, width), BF16),
             jax.ShapeDtypeStruct((1, both + width), F32),
         ),
-        in_specs=[vmem, vmem, vmem, hbm, hbm],
+        in_specs=[vmem, vmem, vmem, vmem, hbm, hbm],
         out_specs=(vmem, vmem),
         scratch_shapes=[
             pltpu.VMEM((depth * experts, both), BF16),
             pltpu.VMEM((both, depth * experts), BF16),
             pltpu.VMEM((fl * experts, width), BF16),
+            pltpu.VMEM((own, 128), F32),
+            pltpu.VMEM((own, 128), BF16),
             pltpu.VMEM((total, depth), BF16),
-            pltpu.VMEM((depth, total), F32),
-            pltpu.VMEM((total, 128), F32),
-            pltpu.VMEM((128, total), F32),
+            pltpu.VMEM((groups, depth, total), F32),
+            pltpu.VMEM((total, 128), BF16),
+            pltpu.VMEM((chunks, total), F32),
+            pltpu.VMEM((chunks, total), F32),
             pltpu.VMEM((depth * experts, total), BF16),
-            pltpu.VMEM((top, both, total), F32),
+            pltpu.VMEM((chunks, both, total), F32),
             pltpu.VMEM((fl, total), F32),
-            pltpu.VMEM((fl * experts, total), F32),
-            pltpu.VMEM((out_chunks, total, width // out_chunks), F32),
+            pltpu.VMEM((groups, fl * experts, span), F32),
+            pltpu.VMEM((groups, span, width), F32),
+            pltpu.VMEM((own, width), F32),
             pltpu.VMEM((n, 1, both + width), F32),
             pltpu.VMEM((n, 1, both + width), F32),
             *hidden_bufs, *hidden_bufs, *out_bufs, *out_bufs,
             pltpu.SemaphoreType.DMA((2,)),
             pltpu.SemaphoreType.DMA((3, n)),
             pltpu.SemaphoreType.DMA((3, n)),
-            pltpu.SemaphoreType.DMA((bits, top)),
-            pltpu.SemaphoreType.DMA((bits, top)),
-            pltpu.SemaphoreType.DMA((bits, out_chunks)),
-            pltpu.SemaphoreType.DMA((bits, out_chunks)),
+            pltpu.SemaphoreType.DMA((bits, chunks)),
+            pltpu.SemaphoreType.DMA((bits, chunks)),
+            pltpu.SemaphoreType.DMA((bits, groups)),
+            pltpu.SemaphoreType.DMA((bits, groups)),
         ],
         compiler_params=pltpu.CompilerParams(
             collective_id=0, has_side_effects=True, vmem_limit_bytes=60 * 2**20
         ),
     )(
         tokens,
-        meta,
+        expert_ids,
+        gate_weights,
         owner_slot.reshape(1, experts),
         gate_up.reshape(depth * experts, both),
         down_proj.reshape(fl * experts, width),

time: 91.2 us -> 87.3 us (0.957)
  Pallas kernels: 85.2 us -> 80.9 us
  local copies, waits for them, and re-layouts: 3.62 us -> 5.5 us
  other arithmetic: 1.37 us -> 0 us
    pallas_call x1, Pallas kernels: 85.2 us -> 80.9 us  [fused(): pl.pallas_call(functools.partial(fused_kernel, (n, bits, chunks, groups))...]
    unnamed x3 -> x4, local copies, waits for them, and re-layouts: 3.54 us -> 5.5 us
where the time goes in v2:
time: 87.3 us; the launch traced here: 87 us
  Pallas kernels  80.9 us (93%)
  local copies, waits for them, and re-layouts  5.5 us (6%)
    pallas_call x1, Pallas kernels, fused(): pl.pallas_call(functools.partial(fused_kernel, (n, bits, chunks, groups))...  80.9 us
    unnamed x4, local copies, waits for them, and re-layouts  5.5 us

profile of v2, /device:TPU:0, one launch (start us, length us, event | category | flops | bytes accessed | tf_op | source)
XLA Modules:
  0.0 87.0 jit_solution(2042268235297125886)
XLA Ops:
  0.6 1.4 %copy.8.ids_ref = s32[16,8]{1,0:T(8,128)} copy(s32[16,8]{0,1:T(8,128)} %param.9) | data formatting | bytes 1024 | tf_op args[3]
  2.0 1.4 %copy.9.gate_ref = f32[16,8]{1,0:T(8,128)} copy(f32[16,8]{0,1:T(8,128)} %param.10) | data formatting | bytes 1024 | tf_op args[4]
  3.3 80.9 %shard_map.77 = (bf16[16,2048]{1,0:T(8,128)(2,1)}, f32[1,3584]{1,0:T(1,128)}) custom-call(bf16[16,2048]{1,0:T(8,128)(2,1)} %tok_ref.1, s32[16,8]{1,0:T(8,128)} %copy.8.ids_ref, f32[16,8]{1,0:T(8,128)} %copy.9.gate_ref, s32[1,16]{1,0:T(1,128)} %bitcast.5, bf16[2048,1536]{1,0:T(8,128)(2,1)} %bitcast.3, bf16[768,2048]{1,0:T(8,128)(2,1)} %bitcast.4), custom_call_target="tpu_custom_call" | custom-call | tf_op jit(solution)/shard_map/pallas_call | solution.py:375
  84.2 1.5 %copy.12 = bf16[16,2048]{1,0:T(8,128)(2,1)} copy(bf16[16,2048]{1,0:T(8,128)(2,1)} %get-tuple-element.4) | data formatting | bytes 131072
  85.7 1.3 %copy.13 = f32[1,3584]{1,0:T(1,128)} copy(f32[1,3584]{1,0:T(1,128)} %get-tuple-element.5) | data formatting | bytes 28672
